TPU v7x, 32 devices: a whole 2x2x4 slice. The times are simulated.
32 devices in a mesh: groups: 2 (over x), expert: 16 (over z, y, core).
Axes of the slice: x: 2, y: 2, z: 4, core: 2. Of those that a mesh axis runs over, the one named last changes fastest.
Arguments:
- queries: bfloat16 [256, 4096], P(('groups', 'expert')), parts along dimension 0, may hold values from -150 to 150
- key_cache: bfloat16 [256, 64, 512], P(('groups', 'expert')), parts along dimension 0, may hold values from -7 to 7
- value_cache: bfloat16 [256, 64, 512], P(('groups', 'expert')), parts along dimension 0, may hold values from -6 to 6
- new_key: bfloat16 [256, 512], P(('groups', 'expert')), parts along dimension 0, may hold values from -6 to 6
- new_value: bfloat16 [256, 512], P(('groups', 'expert')), parts along dimension 0, may hold values from -6 to 6
- cache_lengths: int32 [256], P(('groups', 'expert')), parts along dimension 0, may hold values from 2 to 64, as said below
- hidden_in: bfloat16 [2048, 2048], P(('groups', 'expert')), parts along dimension 0, may hold values from -6 to 6
- norm_gain: bfloat16 [2048], replicated, may hold values from 0.5 to 1.5
- router_weight: bfloat16 [2048, 16], replicated, may hold values from -0.125 to 0.125
- expert_ids: int32 [2048, 8], P(('groups', 'expert')), parts along dimension 0, may hold values from 0 to 15, all different within a row; in each aligned block of 64 rows (0 to 63, 64 to 127, ...) at most 64 rows name the same one
- gate_train: bfloat16 [16, 2048, 768], P(None, 'expert'), may hold values from -0.125 to 0.125
- up_train: bfloat16 [16, 2048, 768], P(None, 'expert'), may hold values from -0.125 to 0.125
- down_train: bfloat16 [16, 768, 2048], P(None, 'expert'), may hold values from -0.21875 to 0.21875
Outputs:
- attended: bfloat16 [256, 4096], P(('groups', 'expert')), parts along dimension 0
- expert_mix: bfloat16 [2048, 2048], P(('groups', 'expert')), parts along dimension 0
There are 2 independent parts, one for each index of `groups`. A program takes and returns all parts, laid end to end along the dimension named above; an argument that names none is the same for every part. Nothing has to cross between parts.
Inputs may be any that keep to these rules, and one draw needn't show every extreme that they name: `expert_ids`: each row names 8 different experts; within the rows of one device no expert is named more than 64 times. `cache_lengths`: the first sequence of each device's 8 has all 64 positions filled.
All inputs are finite; a program needn't handle non-finite values.
Results may differ from a plain program's by a relative error of at most 0.0074.
Values may be sent and summed in bfloat16 or wider, within the bound.
A program may use at most 128 MiB of HBM per device.

v0:
```python
import math
import jax
import jax.numpy as jnp
from jax import lax
from jax.sharding import PartitionSpec as P

HEADS = 32
KV_HEADS = 4
HEAD_DIM = 128
CTX = 64
EPSILON = 1e-06


def rms_normed(hidden_in, norm_gain):
    values = hidden_in.astype(jnp.float32)
    mean_square = jnp.mean(values * values, axis=-1, keepdims=True)
    return (values * lax.rsqrt(mean_square + EPSILON) * norm_gain.astype(jnp.float32)).astype(
        jnp.bfloat16
    )


def attend(queries, key_cache, value_cache, new_key, new_value, cache_lengths):
    seq_count = queries.shape[0]
    group_size = HEADS // KV_HEADS
    query_blocks = queries.reshape(seq_count, KV_HEADS, group_size, HEAD_DIM)
    cached_keys = key_cache.reshape(seq_count, CTX, KV_HEADS, HEAD_DIM)
    cached_values = value_cache.reshape(seq_count, CTX, KV_HEADS, HEAD_DIM)
    fresh_keys = new_key.reshape(seq_count, KV_HEADS, HEAD_DIM)
    fresh_values = new_value.astype(jnp.float32).reshape(seq_count, KV_HEADS, HEAD_DIM)
    score_scale = 1.0 / math.sqrt(HEAD_DIM)
    scores = (
        jnp.einsum("sgrd,scgd->sgrc", query_blocks, cached_keys, preferred_element_type=jnp.float32)
        * score_scale
    )
    own_score = (
        jnp.einsum("sgrd,sgd->sgr", query_blocks, fresh_keys, preferred_element_type=jnp.float32)
        * score_scale
    )
    positions = jnp.arange(CTX, dtype=jnp.int32)
    visible = positions[None, :] < cache_lengths[:, None]
    scores = jnp.where(visible[:, None, None, :], scores, -1e30)
    largest = jnp.maximum(jnp.max(scores, axis=-1), own_score)
    cached_exp = jnp.exp(scores - largest[..., None])
    own_exp = jnp.exp(own_score - largest)
    prob_total = jnp.sum(cached_exp, axis=-1) + own_exp
    cached_prob = (cached_exp / prob_total[..., None]).astype(jnp.bfloat16)
    own_prob = (own_exp / prob_total).astype(jnp.bfloat16).astype(jnp.float32)
    context = jnp.einsum(
        "sgrc,scgd->sgrd", cached_prob, cached_values, preferred_element_type=jnp.float32
    )
    context = context + own_prob[..., None] * fresh_values[:, :, None, :]
    return context.reshape(seq_count, HEADS * HEAD_DIM).astype(jnp.bfloat16)


def expert_rows(received, gate_weight, up_weight, down_weight):
    token_rows = received.reshape(-1, received.shape[2])
    gate_proj = jnp.dot(token_rows, gate_weight, preferred_element_type=jnp.float32)
    up_proj = jnp.dot(token_rows, up_weight, preferred_element_type=jnp.float32)
    hidden_units = (jax.nn.silu(gate_proj) * up_proj).astype(jnp.bfloat16)
    expert_out = jnp.dot(hidden_units, down_weight, preferred_element_type=jnp.float32).astype(
        jnp.bfloat16
    )
    return lax.all_to_all(
        expert_out.reshape(received.shape), "expert", split_axis=0, concat_axis=0, tiled=True
    )


def local(
    queries,
    key_cache,
    value_cache,
    new_key,
    new_value,
    cache_lengths,
    hidden_in,
    norm_gain,
    router_weight,
    expert_ids,
    gate_train,
    up_train,
    down_train,
):
    gate_moved, up_moved, down_moved = (
        lax.all_to_all(gate_train, "expert", split_axis=0, concat_axis=1, tiled=True),
        lax.all_to_all(up_train, "expert", split_axis=0, concat_axis=1, tiled=True),
        lax.all_to_all(down_train, "expert", split_axis=0, concat_axis=1, tiled=True),
    )
    attended = attend(queries, key_cache, value_cache, new_key, new_value, cache_lengths)
    tok_count = hidden_in.shape[0]
    expert_count = router_weight.shape[1]
    top_count = expert_ids.shape[1]
    width = hidden_in.shape[1]
    slot_count = 2 * tok_count * top_count // expert_count
    normed = rms_normed(hidden_in, norm_gain)
    logits = jnp.dot(normed, router_weight, preferred_element_type=jnp.float32)
    expert_range = jnp.arange(expert_count, dtype=jnp.int32)
    picked = expert_ids[:, :, None] == expert_range[None, None, :]
    chosen = jnp.sum(jnp.where(picked, logits[:, None, :], 0.0), axis=-1)
    mixing = jax.nn.softmax(chosen, axis=-1)
    onehot_int = picked.astype(jnp.int32).reshape(-1, expert_count)
    rank_values = jnp.sum((jnp.cumsum(onehot_int, axis=0) - 1) * onehot_int, axis=-1)
    targets = expert_ids.reshape(-1) * slot_count + rank_values
    slot_range = jnp.arange(expert_count * slot_count, dtype=jnp.int32)
    placing = slot_range[:, None] == targets[None, :]
    all_rows, all_ids = (
        lax.all_gather(normed, "expert", axis=0, tiled=True),
        lax.all_gather(expert_ids, "expert", axis=0, tiled=True),
    )
    device_count = lax.axis_size("expert")
    own_index = lax.axis_index("expert")
    own_hits = (all_ids == own_index).astype(jnp.int32).reshape(device_count, tok_count * top_count)
    own_ranks = jnp.cumsum(own_hits, axis=1) - 1
    own_targets = jnp.where(own_hits > 0, own_ranks, -1)
    token_owner = jnp.arange(tok_count * top_count, dtype=jnp.int32) // top_count
    slot_steps = jnp.arange(slot_count, dtype=jnp.int32)
    matches = own_targets[:, None, :] == slot_steps[None, :, None]
    local_token = jnp.sum(jnp.where(matches, token_owner[None, None, :], 0), axis=-1)
    filled = jnp.any(matches, axis=-1)
    row_index = jnp.arange(device_count, dtype=jnp.int32)[:, None] * tok_count + local_token
    taken = jnp.take(all_rows, row_index.reshape(-1), axis=0).reshape(
        device_count, slot_count, width
    )
    received = jnp.where(filled[..., None], taken, jnp.zeros_like(taken))
    returned = expert_rows(received, gate_moved[0], up_moved[0], down_moved[0])
    flat_back = returned.reshape(expert_count * slot_count, width)
    per_assign = lax.dot_general(
        placing.astype(jnp.bfloat16),
        flat_back,
        (((0,), (0,)), ((), ())),
        preferred_element_type=jnp.float32,
    )
    mixed_out = jnp.sum(
        mixing[:, :, None] * per_assign.reshape(tok_count, top_count, width), axis=1
    ).astype(jnp.bfloat16)
    return (attended, mixed_out)


def solution(mesh):
    placed = (
        P(("groups", "expert"), None),
        P(("groups", "expert"), None, None),
        P(("groups", "expert"), None, None),
        P(("groups", "expert"), None),
        P(("groups", "expert"), None),
        P(("groups", "expert")),
        P(("groups", "expert"), None),
        P(),
        P(),
        P(("groups", "expert"), None),
        P(None, "expert", None),
        P(None, "expert", None),
        P(None, "expert", None),
    )
    return jax.shard_map(
        local,
        mesh=mesh,
        in_specs=placed,
        out_specs=(P(("groups", "expert"), None), P(("groups", "expert"), None)),
        check_vma=False,
    )
```

profile of v0, /device:TPU:13, one launch (start us, length us, event | category | flops | bytes accessed | tf_op | source)
XLA Modules:
  0.0 416.2 jit_solution(14784146556622299426)
XLA Ops:
  7.2 0.0 copy-start
  7.2 76.5 %all_to_all.32 = bf16[16,128,768]{2,1,0:T(8,128)(2,1)} all-to-all(bf16[16,128,768]{2,1,0:T(8,128)(2,1)} %param.23), channel_id=1, replica_groups=mesh['groups'=2,'expert'=16] {'expert'}, dimensions={0} | all-to-all | bytes 6291456 | tf_op jit(solution)/shard_map/all_to_all | solution.py:84
  83.7 0.0 copy-start.8
  83.7 0.0 copy-start.2
  83.7 5.2 %all-to-all-start.1 = ((bf16[16,128,768]{2,1,0:T(8,128)(2,1)}), bf16[16,128,768]{2,1,0:T(8,128)(2,1)}, u32[]{:S(2)}, u32[]{:S(2)}) async-start(bf16[16,128,768]{2,1,0:T(8,128)(2,1)} %param.24), calls=%async_computation.1 | async-start | bytes 6291456 | tf_op jit(solution)/shard_map/all_to_all | solution.py:85
  88.9 0.0 all-gather.3.cloned.1.call-start
  89.0 0.0 copy-done.8
  89.0 0.0 copy-done.2
  89.0 0.2 fusion.7
  89.2 0.8 fusion.9
  90.0 0.0 all-gather.3.cloned.1.call-update
  90.0 0.0 copy-start.6
  90.0 94.1 %all-to-all-done.1 = bf16[16,128,768]{2,1,0:T(8,128)(2,1)} async-done(((bf16[16,128,768]{2,1,0:T(8,128)(2,1)}), bf16[16,128,768]{2,1,0:T(8,128)(2,1)}, u32[]{:S(2)}, u32[]{:S(2)}) %all-to-all-start.1) | async-done | bytes 3145760 | tf_op jit(solution)/shard_map/all_to_all | solution.py:85
  184.2 4.8 %all-to-all-start.2 = ((bf16[16,48,2048]{2,1,0:T(8,128)(2,1)}), bf16[16,48,2048]{2,1,0:T(8,128)(2,1)}, u32[]{:S(2)}, u32[]{:S(2)}) async-start(bf16[16,48,2048]{2,1,0:T(8,128)(2,1)} %param.25), calls=%async_computation.2 | async-start | bytes 6291456 | tf_op jit(solution)/shard_map/all_to_all | solution.py:86
  189.0 0.0 copy-done.6
  189.0 79.5 %all-gather = s32[16,64,8]{1,2,0:T(8,128)S(1)} all-gather(s32[1,64,8]{1,2,0:T(8,128)S(1)} %bitcast.77), channel_id=1, replica_groups=mesh['groups'=2,'expert'=16] {'expert'}, dimensions={0}, use_global_device_ids=true | all-gather | bytes 34816 | tf_op jit(solution)/shard_map/all_gather | solution.py:107
  268.5 0.2 copy.59
  268.7 0.2 copy.60
  268.9 0.1 copy.61
  269.0 1.1 reduce-window.16
  270.1 0.2 slice_reduce_fusion
  270.4 0.1 add_add_fusion
  270.5 0.1 copy.67
  270.6 0.1 copy.64
  270.7 0.4 select_reduce_fusion
  271.1 0.1 broadcast_add_fusion
  271.2 0.1 add.101
  271.3 0.1 add.98
  271.3 0.4 fusion
  271.7 0.1 broadcast_in_dim.86
  271.8 0.0 all-gather.3.cloned.1.call-done
  271.9 11.6 %gather_fusion = bf16[1024,2048]{1,0:T(8,128)(2,1)} fusion(bf16[1024,2048]{1,0:T(8,128)(2,1)} %all-gather.3.cloned.1.call-done, s32[1024]{0:T(1024)S(1)} %broadcast_clamp_fusion), kind=kCustom, calls=%fused_computation | custom fusion | bytes 8392704 | tf_op jit(solution)/shard_map/jit(_take)/gather | solution.py:120
  283.4 8.3 %fusion.32 = f32[1024,768]{1,0:T(8,128)} fusion(bf16[2048,768]{1,0:T(8,128)(2,1)} %bitcast.70, bf16[1024,2048]{1,0:T(8,128)(2,1)} %gather_fusion, pred[1024]{0:T(1024)(128)(4,1)S(1)} %compare_and_fusion, pred[1024]{0:T(1024)(128)(4,1)S(1)} %broadcast_in_dim.86), kind=kOutput, calls=%fused_computation.76 | convolution fusion | flops 3225419776 | bytes 10487808 | tf_op jit(solution)/shard_map/dot_general | solution.py:57
  291.7 0.0 all-to-all-done.2
  291.7 13.6 %convolution_convert_fusion = bf16[1024,2048]{1,0:T(8,128)(2,1)} fusion(bf16[768,2048]{1,0:T(8,128)(2,1)} %bitcast.15, f32[1024,768]{1,0:T(8,128)} %fusion.32, bf16[2048,768]{1,0:T(8,128)(2,1)} %bitcast.14, bf16[1024,2048]{1,0:T(8,128)(2,1)} %gather_fusion, pred[1024]{0:T(1024)(128)(4,1)S(1)} %compare_and_fusion, pred[1024]{0:T(1024)(128)(4,1)S(1)} %broadcast_in_dim.86), kind=kOutput, calls=%fused_computation.3 | convolution fusion | flops 6453460992 | bytes 17827840 | tf_op jit(solution)/shard_map/dot_general | solution.py:60
  305.3 0.0 copy-start.7
  305.3 0.0 copy-start.9
  305.3 0.0 copy-start.3
  305.3 5.1 %all-to-all-start.3 = ((bf16[16,64,2048]{2,1,0:T(8,128)(2,1)}), bf16[16,64,2048]{2,1,0:T(8,128)(2,1)}, u32[]{:S(2)}, u32[]{:S(2)}) async-start(bf16[16,64,2048]{2,1,0:T(8,128)(2,1)} %bitcast.69), calls=%async_computation.3 | async-start | bytes 8388608 | tf_op jit(solution)/shard_map/all_to_all | solution.py:63
  310.4 0.0 copy-start.5
  310.4 0.1 copy.56
  310.5 0.1 reshape.285
  310.6 0.1 eq.78
  310.7 0.0 copy-done.7
  310.8 1.2 reduce-window.14
  311.9 0.2 slice_reduce_fusion.1
  312.2 0.0 copy-done.10
  312.2 0.1 iota_compare_fusion.5
  312.2 0.0 copy-done.4
  312.3 0.0 copy-done.9
  312.3 0.2 fusion.17
  312.4 0.0 copy-done.3
  312.4 0.5 fusion.33
  312.9 0.2 fusion.14
  313.2 0.0 copy-done
  313.2 0.3 fusion.5
  313.5 0.7 copy.93
  314.2 0.0 copy-done.1
  314.2 0.0 copy-done.5
  314.2 0.2 fusion.34
  314.4 0.1 copy.55
  314.5 0.1 fusion.21
  314.6 88.7 %all-to-all-done.3 = bf16[16,64,2048]{2,1,0:T(8,128)(2,1)} async-done(((bf16[16,64,2048]{2,1,0:T(8,128)(2,1)}), bf16[16,64,2048]{2,1,0:T(8,128)(2,1)}, u32[]{:S(2)}, u32[]{:S(2)}) %all-to-all-start.3) | async-done | bytes 4194336 | tf_op jit(solution)/shard_map/all_to_all | solution.py:63
  403.4 6.0 %multiply_reduce_fusion = bf16[64,2048]{1,0:T(8,128)(2,1)} fusion(bf16[1024,2048,1]{1,0,2:T(8,128)(2,1)} %bitcast.18, f32[64,8]{1,0:T(8,128)S(1)} %copy.55, s32[512]{0:T(512)S(1)} %multiply_add_fusion), kind=kOutput, calls=%fused_computation.1 | convolution fusion | flops 2149974016 | bytes 4460544 | tf_op jit(solution)/shard_map/dot_general | solution.py:126
  (26 shorter events, 0.3 us)
Async XLA Ops:
  7.2 306.0 %copy-start = (bf16[8,64,512]{2,1,0:T(8,128)(2,1)S(1)}, bf16[8,64,512]{2,1,0:T(8,128)(2,1)}, u32[]{:S(2)}) copy-start(bf16[8,64,512]{2,1,0:T(8,128)(2,1)} %param.15) | copy-start | bytes 1572868
  83.7 5.3 %copy-start.8 = (bf16[2048]{0:T(1024)(128)(2,1)S(1)}, bf16[2048]{0:T(1024)(128)(2,1)}, u32[]{:S(2)}) copy-start(bf16[2048]{0:T(1024)(128)(2,1)} %param.20) | copy-start | bytes 12292
  83.7 5.3 %copy-start.2 = (bf16[64,2048]{1,0:T(8,128)(2,1)S(1)}, bf16[64,2048]{1,0:T(8,128)(2,1)}, u32[]{:S(2)}) copy-start(bf16[64,2048]{1,0:T(8,128)(2,1)} %param.19) | copy-start | bytes 786436
  83.7 100.5 %all-to-all-start.1 = ((bf16[16,128,768]{2,1,0:T(8,128)(2,1)}), bf16[16,128,768]{2,1,0:T(8,128)(2,1)}, u32[]{:S(2)}, u32[]{:S(2)}) async-start(bf16[16,128,768]{2,1,0:T(8,128)(2,1)} %param.24), calls=%async_computation.1 | async-start | bytes 6291456 | tf_op jit(solution)/shard_map/all_to_all | solution.py:85
  88.9 182.9 %all-gather.3.cloned.1.call-start = ((), (), s32[]{:S(2)}) async-start(), calls=%async_computation.4 | async-start | bytes 4456448 | tf_op jit(solution)/shard_map/all_gather | solution.py:106
  90.0 99.0 %copy-start.6 = (s32[64,8]{0,1:T(8,128)S(1)}, s32[64,8]{0,1:T(8,128)}, u32[]{:S(2)}) copy-start(s32[64,8]{0,1:T(8,128)} %param.22) | copy-start | bytes 6148
  184.2 107.5 %all-to-all-start.2 = ((bf16[16,48,2048]{2,1,0:T(8,128)(2,1)}), bf16[16,48,2048]{2,1,0:T(8,128)(2,1)}, u32[]{:S(2)}, u32[]{:S(2)}) async-start(bf16[16,48,2048]{2,1,0:T(8,128)(2,1)} %param.25), calls=%async_computation.2 | async-start | bytes 6291456 | tf_op jit(solution)/shard_map/all_to_all | solution.py:86
  305.3 5.4 %copy-start.7 = (bf16[8,512]{1,0:T(8,128)(2,1)S(1)}, bf16[8,512]{1,0:T(8,128)(2,1)}, u32[]{:S(2)}) copy-start(bf16[8,512]{1,0:T(8,128)(2,1)} %param.17) | copy-start | bytes 24580
  305.3 6.9 %copy-start.10 = (s32[8]{0:T(128)S(1)}, s32[8]{0:T(128)}, u32[]{:S(2)}) copy-start(s32[8]{0:T(128)} %param.18) | copy-start | bytes 100
  305.3 7.0 %copy-start.4 = (bf16[8,4096]{1,0:T(8,128)(2,1)S(1)}, bf16[8,4096]{1,0:T(8,128)(2,1)}, u32[]{:S(2)}) copy-start(bf16[8,4096]{1,0:T(8,128)(2,1)} %param.13) | copy-start | bytes 196612
  305.3 7.0 %copy-start.9 = (bf16[8,512]{1,0:T(8,128)(2,1)S(1)}, bf16[8,512]{1,0:T(8,128)(2,1)}, u32[]{:S(2)}) copy-start(bf16[8,512]{1,0:T(8,128)(2,1)} %param.16) | copy-start | bytes 24580
  305.3 7.1 %copy-start.3 = (bf16[8,64,512]{2,1,0:T(8,128)(2,1)S(1)}, bf16[8,64,512]{2,1,0:T(8,128)(2,1)}, u32[]{:S(2)}) copy-start(bf16[8,64,512]{2,1,0:T(8,128)(2,1)} %param.14) | copy-start | bytes 1572868
  305.3 98.1 %all-to-all-start.3 = ((bf16[16,64,2048]{2,1,0:T(8,128)(2,1)}), bf16[16,64,2048]{2,1,0:T(8,128)(2,1)}, u32[]{:S(2)}, u32[]{:S(2)}) async-start(bf16[16,64,2048]{2,1,0:T(8,128)(2,1)} %bitcast.69), calls=%async_computation.3 | async-start | bytes 8388608 | tf_op jit(solution)/shard_map/all_to_all | solution.py:63
  310.4 3.7 copy-start.1
  310.4 3.7 copy-start.5
Sparse Core Ops, SparseCore 0:
  92.5 77.4 all-gather.2
where the time goes:
time: 417 us; the launch traced here: 416 us
  waiting for transfers between devices  183 us (44%)
  blocking collectives  156 us (37%)
  matrix products  28.9 us (7%)
  starting transfers between devices  15.2 us (4%)
  between operations  14.3 us (3%)
  local copies, waits for them, and re-layouts  14 us (3%)
  other arithmetic  4.86 us (1%)
    all_to_all x1, waiting for transfers between devices, local(): lax.all_to_all(up_train, 'expert', split_axis=0, concat_axis=1, tiled=True)  94.1 us
    all_to_all x1, waiting for transfers between devices, expert_rows(): lax.all_to_all(expert_out.reshape(received.shape), 'expert', split_axis=0...  88.7 us
    all_gather x1, blocking collectives, local(): lax.all_gather(expert_ids, 'expert', axis=0, tiled=True)  79.5 us
    all_to_all x1, blocking collectives, local(): lax.all_to_all(gate_train, 'expert', split_axis=0, concat_axis=1, tiled=T...  76.5 us
    dot_general x1, matrix products, expert_rows(): jnp.dot(hidden_units, down_weight, preferred_element_type=jnp.float32)  13.6 us
    gather x1, local copies, waits for them, and re-layouts, local(): jnp.take(all_rows, row_index.reshape(-1), axis=0)  11.6 us
  transfers between devices with their start and end apart: 4, of which 2 were waited for; matrix products, arithmetic and copies ran while one was open for 7% of the time, Pallas kernels for 0%

commit v1 on v0

--- a/solution.py
+++ b/solution.py
@@ -9,6 +9,11 @@
 HEAD_DIM = 128
 CTX = 64
 EPSILON = 1e-06
+
+
+def swapped_in(block, axis, dim):
+    sent = jnp.stack([block] * lax.axis_size(axis))
+    return jnp.concatenate(lax.all_to_all(sent, axis, 0, 0), axis=dim)
 
 
 def rms_normed(hidden_in, norm_gain):
@@ -104,7 +109,7 @@
     placing = slot_range[:, None] == targets[None, :]
     all_rows, all_ids = (
         lax.all_gather(normed, "expert", axis=0, tiled=True),
-        lax.all_gather(expert_ids, "expert", axis=0, tiled=True),
+        swapped_in(expert_ids, "expert", 0),
     )
     device_count = lax.axis_size("expert")
     own_index = lax.axis_index("expert")

time: 417 us -> 395 us (0.947)
  blocking collectives: 156 us -> 87.2 us
  waiting for transfers between devices: 183 us -> 228 us
    all_gather x1 -> x0, blocking collectives: 79.5 us -> none  [local(): lax.all_gather(expert_ids, 'expert', axis=0, tiled=True)]
    all_to_all x1, waiting for transfers between devices: 0.01 us -> 45.5 us  [local(): lax.all_to_all(down_train, 'expert', split_axis=0, concat_axis=1, tiled=T...]
    all_to_all x0 -> x1, blocking collectives: none -> 10.5 us  [swapped_in(): return jnp.concatenate(lax.all_to_all(sent, axis, 0, 0), axis=dim)]
  transfers between devices with their start and end apart: 4 -> 4, of which waited for: 2 -> 3; matrix products, arithmetic and copies ran while one was open for 7% -> 7% of each run, Pallas kernels for 0% -> 0%
where the time goes in v1:
time: 395 us; the launch traced here: 394 us
  waiting for transfers between devices  228 us (58%)
  blocking collectives  87.2 us (22%)
  matrix products  28.9 us (7%)
  local copies, waits for them, and re-layouts  15.4 us (4%)
  starting transfers between devices  14.8 us (4%)
  between operations  14.3 us (4%)
  other arithmetic  5.57 us (1%)
    all_to_all x1, waiting for transfers between devices, local(): lax.all_to_all(up_train, 'expert', split_axis=0, concat_axis=1, tiled=True)  94.1 us
    all_to_all x1, waiting for transfers between devices, expert_rows(): lax.all_to_all(expert_out.reshape(received.shape), 'expert', split_axis=0...  88.2 us
    all_to_all x1, blocking collectives, local(): lax.all_to_all(gate_train, 'expert', split_axis=0, concat_axis=1, tiled=T...  76.7 us
    all_to_all x1, waiting for transfers between devices, local(): lax.all_to_all(down_train, 'expert', split_axis=0, concat_axis=1, tiled=T...  45.5 us
    dot_general x1, matrix products, expert_rows(): jnp.dot(hidden_units, down_weight, preferred_element_type=jnp.float32)  13.6 us
    gather x1, local copies, waits for them, and re-layouts, local(): jnp.take(all_rows, row_index.reshape(-1), axis=0)  11.6 us
    all_to_all x1, blocking collectives, swapped_in(): return jnp.concatenate(lax.all_to_all(sent, axis, 0, 0), axis=dim)  10.5 us
    dot_general x1, matrix products, expert_rows(): jnp.dot(token_rows, gate_weight, preferred_element_type=jnp.float32)  8.28 us
  transfers between devices with their start and end apart: 4, of which 3 were waited for; matrix products, arithmetic and copies ran while one was open for 7% of the time, Pallas kernels for 0%

profile of v1, /device:TPU:13, one launch (start us, length us, event | category | flops | bytes accessed | tf_op | source)
XLA Modules:
  0.0 394.1 jit_solution(12866931326653211074)
XLA Ops:
  7.2 0.0 copy-start
  7.2 0.8 broadcast_bitcast_fusion
  7.9 0.1 reshape.318
  8.0 10.5 %all_to_all.37 = s32[16,1,512]{2,1,0:T(1,128)S(1)} all-to-all(s32[16,1,512]{2,1,0:T(1,128)S(1)} %reshape.318), channel_id=1, replica_groups=mesh['groups'=2,'expert'=16] {'expert'}, dimensions={0} | all-to-all | bytes 65536 | tf_op jit(solution)/shard_map/all_to_all | solution.py:16
  18.5 76.7 %all_to_all.38 = bf16[16,128,768]{2,1,0:T(8,128)(2,1)} all-to-all(bf16[16,128,768]{2,1,0:T(8,128)(2,1)} %param.23), channel_id=1, replica_groups=mesh['groups'=2,'expert'=16] {'expert'}, dimensions={0} | all-to-all | bytes 6291456 | tf_op jit(solution)/shard_map/all_to_all | solution.py:89
  95.2 5.0 %all-to-all-start.2 = ((bf16[16,128,768]{2,1,0:T(8,128)(2,1)}), bf16[16,128,768]{2,1,0:T(8,128)(2,1)}, u32[]{:S(2)}, u32[]{:S(2)}) async-start(bf16[16,128,768]{2,1,0:T(8,128)(2,1)} %param.24), calls=%async_computation.2 | async-start | bytes 6291456 | tf_op jit(solution)/shard_map/all_to_all | solution.py:90
  100.2 0.0 all-gather.2.cloned.1.call-start
  100.3 0.0 copy-done.8
  100.3 0.0 copy-done.2
  100.3 0.2 fusion.7
  100.5 0.8 fusion.9
  101.3 0.0 all-gather.2.cloned.1.call-update
  101.3 94.1 %all-to-all-done.2 = bf16[16,128,768]{2,1,0:T(8,128)(2,1)} async-done(((bf16[16,128,768]{2,1,0:T(8,128)(2,1)}), bf16[16,128,768]{2,1,0:T(8,128)(2,1)}, u32[]{:S(2)}, u32[]{:S(2)}) %all-to-all-start.2) | async-done | bytes 3145760 | tf_op jit(solution)/shard_map/all_to_all | solution.py:90
  195.5 4.8 %all-to-all-start.3 = ((bf16[16,48,2048]{2,1,0:T(8,128)(2,1)}), bf16[16,48,2048]{2,1,0:T(8,128)(2,1)}, u32[]{:S(2)}, u32[]{:S(2)}) async-start(bf16[16,48,2048]{2,1,0:T(8,128)(2,1)} %param.25), calls=%async_computation.3 | async-start | bytes 6291456 | tf_op jit(solution)/shard_map/all_to_all | solution.py:91
  200.3 0.5 broadcast.248
  200.8 0.7 reduce.4
  201.5 0.1 reshape.319
  201.6 0.2 copy.59
  201.8 0.2 copy.60
  202.0 0.1 copy.61
  202.1 1.1 reduce-window.16
  203.2 0.2 slice_reduce_fusion
  203.5 0.1 add_add_fusion
  203.6 0.1 copy.67
  203.7 0.1 copy.64
  203.8 0.4 select_reduce_fusion
  204.2 0.1 broadcast_add_fusion
  204.3 0.1 add.101
  204.4 0.1 add.98
  204.4 0.4 fusion
  204.8 0.1 broadcast_in_dim.86
  204.9 0.0 all-gather.2.cloned.1.call-done
  204.9 11.6 %gather_fusion = bf16[1024,2048]{1,0:T(8,128)(2,1)} fusion(bf16[1024,2048]{1,0:T(8,128)(2,1)} %all-gather.2.cloned.1.call-done, s32[1024]{0:T(1024)S(1)} %broadcast_clamp_fusion), kind=kCustom, calls=%fused_computation | custom fusion | bytes 8392704 | tf_op jit(solution)/shard_map/jit(_take)/gather | solution.py:125
  216.5 8.3 %fusion.32 = f32[1024,768]{1,0:T(8,128)} fusion(bf16[2048,768]{1,0:T(8,128)(2,1)} %bitcast.73, bf16[1024,2048]{1,0:T(8,128)(2,1)} %gather_fusion, pred[1024]{0:T(1024)(128)(4,1)S(1)} %compare_and_fusion, pred[1024]{0:T(1024)(128)(4,1)S(1)} %broadcast_in_dim.86), kind=kOutput, calls=%fused_computation.76 | convolution fusion | flops 3225419776 | bytes 10487808 | tf_op jit(solution)/shard_map/dot_general | solution.py:62
  224.8 45.5 %all-to-all-done.3 = bf16[16,48,2048]{2,1,0:T(8,128)(2,1)} async-done(((bf16[16,48,2048]{2,1,0:T(8,128)(2,1)}), bf16[16,48,2048]{2,1,0:T(8,128)(2,1)}, u32[]{:S(2)}, u32[]{:S(2)}) %all-to-all-start.3) | async-done | bytes 3145760 | tf_op jit(solution)/shard_map/all_to_all | solution.py:91
  270.3 13.6 %convolution_convert_fusion = bf16[1024,2048]{1,0:T(8,128)(2,1)} fusion(bf16[768,2048]{1,0:T(8,128)(2,1)} %bitcast.14, f32[1024,768]{1,0:T(8,128)} %fusion.32, bf16[2048,768]{1,0:T(8,128)(2,1)} %bitcast.13, bf16[1024,2048]{1,0:T(8,128)(2,1)} %gather_fusion, pred[1024]{0:T(1024)(128)(4,1)S(1)} %compare_and_fusion, pred[1024]{0:T(1024)(128)(4,1)S(1)} %broadcast_in_dim.86), kind=kOutput, calls=%fused_computation.3 | convolution fusion | flops 6453460992 | bytes 17827840 | tf_op jit(solution)/shard_map/dot_general | solution.py:65
  283.9 0.0 copy-start.4
  283.9 0.0 copy-start.9
  283.9 0.0 copy-start.3
  283.9 4.9 %all-to-all-start.4 = ((bf16[16,64,2048]{2,1,0:T(8,128)(2,1)}), bf16[16,64,2048]{2,1,0:T(8,128)(2,1)}, u32[]{:S(2)}, u32[]{:S(2)}) async-start(bf16[16,64,2048]{2,1,0:T(8,128)(2,1)} %bitcast.72), calls=%async_computation.4 | async-start | bytes 8388608 | tf_op jit(solution)/shard_map/all_to_all | solution.py:68
  288.8 0.0 copy-done.6
  288.8 0.0 copy-start.1
  288.8 0.0 copy-start.5
  288.8 0.1 copy.56
  288.9 0.1 reshape.298
  289.0 0.1 eq.86
  289.1 0.0 copy-done.7
  289.2 1.2 reduce-window.14
  290.3 0.2 slice_reduce_fusion.1
  290.6 0.0 copy-done.10
  290.6 0.1 iota_compare_fusion.5
  290.6 0.0 copy-done.4
  290.7 0.0 copy-done.9
  290.7 0.2 fusion.17
  290.8 0.5 fusion.33
  291.3 0.2 fusion.14
  291.6 0.3 fusion.5
  291.9 0.7 copy.93
  292.6 0.0 copy-done.5
  292.6 0.2 fusion.34
  292.8 0.1 copy.55
  292.9 0.1 fusion.21
  293.0 88.2 %all-to-all-done.4 = bf16[16,64,2048]{2,1,0:T(8,128)(2,1)} async-done(((bf16[16,64,2048]{2,1,0:T(8,128)(2,1)}), bf16[16,64,2048]{2,1,0:T(8,128)(2,1)}, u32[]{:S(2)}, u32[]{:S(2)}) %all-to-all-start.4) | async-done | bytes 4194336 | tf_op jit(solution)/shard_map/all_to_all | solution.py:68
  381.3 6.0 %multiply_reduce_fusion = bf16[64,2048]{1,0:T(8,128)(2,1)} fusion(bf16[1024,2048,1]{1,0,2:T(8,128)(2,1)} %bitcast.17, f32[64,8]{1,0:T(8,128)S(1)} %copy.55, s32[512]{0:T(512)S(1)} %multiply_add_fusion), kind=kOutput, calls=%fused_computation.1 | convolution fusion | flops 2149974016 | bytes 4460544 | tf_op jit(solution)/shard_map/dot_general | solution.py:131
  (31 shorter events, 0.3 us)
Async XLA Ops:
  7.2 284.4 %copy-start = (bf16[8,64,512]{2,1,0:T(8,128)(2,1)S(1)}, bf16[8,64,512]{2,1,0:T(8,128)(2,1)}, u32[]{:S(2)}) copy-start(bf16[8,64,512]{2,1,0:T(8,128)(2,1)} %param.15) | copy-start | bytes 1572868
  95.2 5.1 %copy-start.8 = (bf16[2048]{0:T(1024)(128)(2,1)S(1)}, bf16[2048]{0:T(1024)(128)(2,1)}, u32[]{:S(2)}) copy-start(bf16[2048]{0:T(1024)(128)(2,1)} %param.20) | copy-start | bytes 12292
  95.2 5.1 %copy-start.2 = (bf16[64,2048]{1,0:T(8,128)(2,1)S(1)}, bf16[64,2048]{1,0:T(8,128)(2,1)}, u32[]{:S(2)}) copy-start(bf16[64,2048]{1,0:T(8,128)(2,1)} %param.19) | copy-start | bytes 786436
  95.2 100.2 %all-to-all-start.2 = ((bf16[16,128,768]{2,1,0:T(8,128)(2,1)}), bf16[16,128,768]{2,1,0:T(8,128)(2,1)}, u32[]{:S(2)}, u32[]{:S(2)}) async-start(bf16[16,128,768]{2,1,0:T(8,128)(2,1)} %param.24), calls=%async_computation.2 | async-start | bytes 6291456 | tf_op jit(solution)/shard_map/all_to_all | solution.py:90
  100.2 104.7 %all-gather.2.cloned.1.call-start = ((), (), s32[]{:S(2)}) async-start(), calls=%async_computation.5 | async-start | bytes 4456448 | tf_op jit(solution)/shard_map/all_gather | solution.py:111
  195.5 74.8 %all-to-all-start.3 = ((bf16[16,48,2048]{2,1,0:T(8,128)(2,1)}), bf16[16,48,2048]{2,1,0:T(8,128)(2,1)}, u32[]{:S(2)}, u32[]{:S(2)}) async-start(bf16[16,48,2048]{2,1,0:T(8,128)(2,1)} %param.25), calls=%async_computation.3 | async-start | bytes 6291456 | tf_op jit(solution)/shard_map/all_to_all | solution.py:91
  283.8 5.0 %copy-start.6 = (s32[64,8]{0,1:T(8,128)S(1)}, s32[64,8]{0,1:T(8,128)}, u32[]{:S(2)}) copy-start(s32[64,8]{0,1:T(8,128)} %param.22) | copy-start | bytes 6148
  283.8 5.3 %copy-start.7 = (bf16[8,512]{1,0:T(8,128)(2,1)S(1)}, bf16[8,512]{1,0:T(8,128)(2,1)}, u32[]{:S(2)}) copy-start(bf16[8,512]{1,0:T(8,128)(2,1)} %param.17) | copy-start | bytes 24580
  283.9 6.7 %copy-start.10 = (s32[8]{0:T(128)S(1)}, s32[8]{0:T(128)}, u32[]{:S(2)}) copy-start(s32[8]{0:T(128)} %param.18) | copy-start | bytes 100
  283.9 6.8 %copy-start.4 = (bf16[8,4096]{1,0:T(8,128)(2,1)S(1)}, bf16[8,4096]{1,0:T(8,128)(2,1)}, u32[]{:S(2)}) copy-start(bf16[8,4096]{1,0:T(8,128)(2,1)} %param.13) | copy-start | bytes 196612
  283.9 6.8 %copy-start.9 = (bf16[8,512]{1,0:T(8,128)(2,1)S(1)}, bf16[8,512]{1,0:T(8,128)(2,1)}, u32[]{:S(2)}) copy-start(bf16[8,512]{1,0:T(8,128)(2,1)} %param.16) | copy-start | bytes 24580
  283.9 6.9 %copy-start.3 = (bf16[8,64,512]{2,1,0:T(8,128)(2,1)S(1)}, bf16[8,64,512]{2,1,0:T(8,128)(2,1)}, u32[]{:S(2)}) copy-start(bf16[8,64,512]{2,1,0:T(8,128)(2,1)} %param.14) | copy-start | bytes 1572868
  283.9 97.4 %all-to-all-start.4 = ((bf16[16,64,2048]{2,1,0:T(8,128)(2,1)}), bf16[16,64,2048]{2,1,0:T(8,128)(2,1)}, u32[]{:S(2)}, u32[]{:S(2)}) async-start(bf16[16,64,2048]{2,1,0:T(8,128)(2,1)} %bitcast.72), calls=%async_computation.4 | async-start | bytes 8388608 | tf_op jit(solution)/shard_map/all_to_all | solution.py:68
  288.8 3.7 copy-start.1
  288.8 3.7 copy-start.5
Sparse Core Ops, SparseCore 0:
  103.8 77.4 all-gather.1
